TPU v7x, 128 devices: a whole 4x4x4 slice. The times are simulated.
128 devices in a mesh: row: 4 (over y), col: 4 (over z), depth: 8 (over x, core).
Axes of the slice: x: 4, y: 4, z: 4, core: 2. Of those that a mesh axis runs over, the one named last changes fastest.
Arguments:
- diag_block: float32 [512, 512], P(('row', 'col', 'depth')), as said below
- panel_rows: float32 [32256, 512], P(('row', 'col', 'depth')), may hold values from -2 to 2
- trailing: float32 [32256, 1024], P(('row', 'depth'), 'col'), may hold values from -6 to 6
Outputs:
- diag_factor: float32 [512, 512], P(('row', 'col', 'depth'))
- panel_factor: float32 [32256, 512], P(('row', 'col', 'depth'))
- updated: float32 [32256, 1024], P(('row', 'depth'), 'col')
Inputs may be any that keep to these rules, and one draw needn't show every extreme that they name: `diag_block`: symmetric positive definite.
All inputs are finite; a program needn't handle non-finite values.
Results may differ from a plain program's by a relative error of at most 0.000062.
Values sent between devices are 32-bit elements; how exact they have to be, the bound alone decides.
A program may use at most 64 MiB of HBM per device.

v0:
```python
import jax
import jax.numpy as jnp
from jax import lax
from jax.experimental import pallas as pl
from jax.experimental.pallas import tpu as pltpu
from jax.sharding import Mesh
from jax.sharding import PartitionSpec as P

DEPTH = ("depth_0", "depth_1")
ROW_COL_DEPTH = ("row", "col", "depth_0", "depth_1")
ROW_DEPTH = ("row", "depth_0", "depth_1")


F32 = jnp.float32
NT = (((1,), (1,)), ((), ()))
BLOCK = 128


def lane(v, j):
    return jnp.broadcast_to(v[:, j : j + 1], (8, 128))


def sub(v, k):
    return jnp.broadcast_to(v[k : k + 1, :], (8, 128))


def split(x):
    hi = x.astype(jnp.bfloat16)
    return hi, (x - hi.astype(F32)).astype(jnp.bfloat16)


def dot(a, b):
    def one(x, y):
        return lax.dot_general(x, y, NT, preferred_element_type=F32)

    return one(a[0], b[0]) + (one(a[0], b[1]) + one(a[1], b[0]))


def factor_block(rows):
    ri = lax.broadcasted_iota(jnp.int32, (8, 128), 0)
    li = lax.broadcasted_iota(jnp.int32, (8, 128), 1)
    rows = list(rows)
    unit = [jnp.where(li == ri + 8 * v, 1.0, 0.0).astype(F32) for v in range(16)]
    upper, inverse = [], []
    for p in range(16):
        n = 16 - p
        cols = [[lane(rows[p + v], 8 * p + j) for j in range(8)] for v in range(n)]
        r = [sub(rows[p], k) for k in range(8)]
        s = [sub(unit[p], k) for k in range(8)]
        for k in range(8):
            inv = lax.rsqrt(sub(cols[0][k], k))
            for v in range(n):
                cols[v][k] = cols[v][k] * inv
            r[k] = r[k] * inv
            s[k] = s[k] * inv
            for j in range(k + 1, 8):
                m = sub(cols[0][k], j)
                for v in range(n):
                    cols[v][j] = cols[v][j] - cols[v][k] * m
                r[j] = r[j] - m * r[k]
                s[j] = s[j] - m * s[k]
        u, t = r[0], s[0]
        for k in range(1, 8):
            u = jnp.where(ri == k, r[k], u)
            t = jnp.where(ri == k, s[k], t)
        upper.append(jnp.where(li >= ri + 8 * p, u, 0.0))
        inverse.append(t)
        for v in range(1, n):
            for k in range(8):
                rows[p + v] = rows[p + v] - cols[v][k] * r[k]
                unit[p + v] = unit[p + v] - cols[v][k] * s[k]
    return upper, inverse


def at(i):
    return slice(BLOCK * i, BLOCK * (i + 1))


def factor_all(a_ref, l_ref, s_ref, lows, invs):
    n = 4
    for k in range(n):
        src = a_ref if k == 0 else s_ref
        upper, inverse = factor_block(
            [src[BLOCK * k + 8 * v : BLOCK * k + 8 * v + 8, at(k)] for v in range(16)]
        )
        invs[k] = split(jnp.concatenate(inverse, 0))
        l_ref[at(k), at(k)] = jnp.concatenate(upper, 0).T
        for j in range(k + 1, n):
            l_ref[at(k), at(j)] = jnp.zeros((BLOCK, BLOCK), F32)
        for i in range(k + 1, n):
            low = dot(split(src[at(i), at(k)]), invs[k])
            l_ref[at(i), at(k)] = low
            lows[i, k] = split(low)
        for i in range(k + 1, n):
            for j in range(k + 1, i + 1):
                s_ref[at(i), at(j)] = src[at(i), at(j)] - dot(lows[i, k], lows[j, k])


def solve(x, lows, invs):
    done = []
    for k in range(4):
        acc = x[:, at(k)]
        for m in range(k):
            acc = acc - dot(done[m][1], lows[k, m])
        value = dot(split(acc), invs[k])
        done.append((value, split(value)))
    return done


def product(a, b):
    total = dot(a[0][1], b[0][1])
    for k in range(1, 4):
        total = total + dot(a[k][1], b[k][1])
    return total


def compute(diag, own, rows, window, trailing, own_l, solved, updated, l_ref, s_ref):
    lows, invs = {}, {}
    factor_all(diag, l_ref, s_ref, lows, invs)
    position = lax.axis_index("row") * 32 + lax.axis_index("col") * 8 + lax.axis_index(DEPTH)
    pair = l_ref[pl.ds(pl.multiple_of((position // 2) * 8, 8), 8), :]
    own_l[...] = jnp.where(position % 2 == 0, pair[0:4], pair[4:8])
    w = solve(window[...], lows, invs)
    for k, (value, _) in enumerate(solve(own[...], lows, invs)):
        solved[:, at(k)] = value
    size = own.shape[0]
    for j in range(4):
        span = slice(size * j, size * (j + 1))
        x = solve(rows[span, :], lows, invs)
        updated[span, :] = trailing[span, :] - product(x, w)


def all_compute(diag, own, rows, window, trailing):
    spec = pl.BlockSpec(memory_space=pltpu.VMEM)
    return pl.pallas_call(
        compute,
        out_shape=(
            jax.ShapeDtypeStruct((4, 512), F32),
            jax.ShapeDtypeStruct(own.shape, F32),
            jax.ShapeDtypeStruct(trailing.shape, F32),
        ),
        in_specs=[spec] * 5,
        out_specs=(spec,) * 3,
        scratch_shapes=[pltpu.VMEM((512, 512), F32), pltpu.VMEM((512, 512), F32)],
        compiler_params=pltpu.CompilerParams(vmem_limit_bytes=48 * 2**20),
        name="factor_solve_update",
    )(diag, own, rows, window, trailing)


def sent_to_all(value, axis):
    copies = jnp.broadcast_to(value, (lax.axis_size(axis), *value.shape))
    return lax.all_to_all(copies, axis, split_axis=0, concat_axis=0, tiled=True)


def in_order(tiles, dim):
    shape = list(tiles.shape[1:])
    shape[dim] *= tiles.shape[0]
    return jnp.moveaxis(tiles, 0, dim).reshape(shape)


def gather_directly(value, axis, dim):
    tiles = sent_to_all(value, axis)
    return in_order(tiles, dim)


def broadcast(value, axis, root):
    return lax.dynamic_index_in_dim(lax.all_gather(value, axis), root, 0, keepdims=False)


def gather_axes(value, axes, dim):
    far, near = axes
    tiles = sent_to_all(sent_to_all(value, far), near)
    return in_order(tiles.swapaxes(0, 1).reshape(-1, *value.shape), dim)


def gathered_by_axis(value, axes, dim):
    if not axes:
        return value
    nearer = lax.all_gather(value, axes[-1], axis=dim, tiled=True)
    return gathered_by_axis(nearer, axes[:-1], dim)


def split_panel(solved, win_rows):
    ranges = lax.all_to_all(solved, DEPTH, split_axis=1, concat_axis=0, tiled=True)
    row_panel = gather_directly(ranges, "col", 0)
    local_window = lax.dynamic_slice_in_dim(
        row_panel, lax.axis_index("col") * win_rows, win_rows, 0
    )
    window = broadcast(local_window, "row", 0)
    return (row_panel, window)


def body(diag_block, panel_rows, trailing):
    whole_diag = gather_axes(diag_block, (("row", "col", "depth_0"), "depth_1"), 0)
    row_panel, window = split_panel(panel_rows, trailing.shape[1])
    owned = lax.all_to_all(row_panel, DEPTH, split_axis=0, concat_axis=1, tiled=True)
    full_window = gathered_by_axis(window, DEPTH, 1)
    return all_compute(whole_diag, panel_rows, owned, full_window, trailing)


def solution(mesh):
    split = Mesh(
        mesh.devices.reshape(mesh.shape["row"], mesh.shape["col"], 4, 2),
        ("row", "col", "depth_0", "depth_1"),
    )
    return jax.shard_map(
        body,
        mesh=split,
        in_specs=(P(ROW_COL_DEPTH, None), P(ROW_COL_DEPTH, None), P(ROW_DEPTH, "col")),
        out_specs=(P(ROW_COL_DEPTH, None), P(ROW_COL_DEPTH, None), P(ROW_DEPTH, "col")),
        check_vma=False,
    )
```

profile of v0, /device:TPU:1, one launch (start us, length us, event | category | flops | bytes accessed | tf_op | source)
XLA Modules:
  0.0 152.5 jit_solution(15694604143050432222)
XLA Ops:
  0.6 0.0 copy-start.3
  0.6 1.2 copy.24
  1.9 14.9 %all_to_all.53 = f32[252,8,64]{0,2,1:T(8,128)S(1)} all-to-all(f32[252,8,64]{0,2,1:T(8,128)S(1)} %bitcast.14), channel_id=1, replica_groups=mesh['row'=4,'col'=4,'depth_0'=4,'depth_1'=2] {'depth_0','depth_1'}, dimensions={1} | all-to-all | bytes 1032192 | tf_op jit(solution)/shard_map/all_to_all | solution.py:184
  16.8 0.0 copy-done.3
  16.8 0.9 broadcast_in_dim.9
  17.7 9.3 %all-to-all-start = ((f32[64,4,512]{2,1,0:T(4,128)}), f32[64,4,512]{2,1,0:T(4,128)S(1)}, u32[]{:S(2)}, u32[]{:S(2)}) async-start(f32[64,4,512]{2,1,0:T(4,128)} %broadcast_in_dim.9), calls=%async_computation | async-start | bytes 1048576 | tf_op jit(solution)/shard_map/all_to_all | solution.py:152
  26.9 0.3 copy.25
  27.3 0.2 all_to_all.42
  27.5 11.3 %all-to-all-done = f32[64,4,512]{2,1,0:T(4,128)S(1)} async-done(((f32[64,4,512]{2,1,0:T(4,128)}), f32[64,4,512]{2,1,0:T(4,128)S(1)}, u32[]{:S(2)}, u32[]{:S(2)}) %all-to-all-start) | async-done | bytes 524320 | tf_op jit(solution)/shard_map/all_to_all | solution.py:152
  38.8 0.2 broadcast_in_dim.11
  39.1 27.2 %all_to_all.54 = f32[4,2016,64]{1,2,0:T(8,128)} all-to-all(f32[4,2016,64]{1,2,0:T(8,128)S(1)} %broadcast_in_dim.11), channel_id=1, replica_groups=mesh['row'=4,'col'=4,'depth_0'=4,'depth_1'=2] {'col'}, dimensions={0} | all-to-all | bytes 4128768 | tf_op jit(solution)/shard_map/all_to_all | solution.py:152
  66.2 1.1 broadcast_in_dim.10
  67.3 6.9 %all-to-all-start.1 = ((f32[2,64,4,512]{3,2,1,0:T(4,128)}), f32[2,64,4,512]{3,2,1,0:T(4,128)S(1)}, u32[]{:S(2)}, u32[]{:S(2)}) async-start(f32[2,64,4,512]{3,2,1,0:T(4,128)} %broadcast_in_dim.10), calls=%async_computation.1 | async-start | bytes 2097152 | tf_op jit(solution)/shard_map/all_to_all | solution.py:152
  74.3 2.9 %copy.26 = f32[4,2016,64]{1,0,2:T(4,128)S(1)} copy(f32[4,2016,64]{1,2,0:T(8,128)} %all_to_all.54) | data formatting | bytes 4128768 | tf_op jit(solution)/shard_map/all_to_all | solution.py:152
  77.2 2.0 %all_to_all.44 = f32[8,1008,64]{1,0,2:T(8,128)} reshape(f32[4,2016,64]{1,0,2:T(4,128)S(1)} %copy.26) | data formatting | bytes 4128768 | tf_op jit(solution)/shard_map/all_to_all | solution.py:196
  79.2 4.1 %copy.27 = f32[8,1008,64]{1,2,0:T(8,128)} copy(f32[8,1008,64]{1,0,2:T(8,128)} %all_to_all.44) | data formatting | bytes 4128768 | tf_op jit(solution)/shard_map/all_to_all | solution.py:196
  83.4 0.0 all-to-all-done.1
  83.4 4.3 %all-to-all-start.4 = ((f32[8,1008,64]{1,2,0:T(8,128)}), f32[8,1008,64]{1,2,0:T(8,128)}, u32[]{:S(2)}, u32[]{:S(2)}) async-start(f32[8,1008,64]{1,2,0:T(8,128)} %copy.27), calls=%async_computation.4 | async-start | bytes 4194304 | tf_op jit(solution)/shard_map/all_to_all | solution.py:196
  87.7 1.1 copy.23
  88.8 1.6 %reshape_reshape.3.diag = f32[512,512]{1,0:T(8,128)S(1)} reshape(f32[64,2,4,512]{3,2,1,0:T(4,128)} %copy.23) | data formatting | bytes 2097152 | tf_op jit(solution)/shard_map/reshape;reshape | solution.py:158
  90.4 3.3 %reshape.16 = f32[8064,64]{0,1:T(8,128)} reshape(f32[4,2016,64]{1,0,2:T(4,128)S(1)} %copy.26) | data formatting | bytes 4128768 | tf_op jit(solution)/shard_map/reshape | solution.py:158
  93.6 0.8 constant_dynamic-slice_fusion
  94.5 10.2 %all-gather = f32[1024,64]{0,1:T(8,128)S(1)} all-gather(f32[256,64]{0,1:T(8,128)S(1)} %constant_dynamic-slice_fusion), channel_id=2, replica_groups=mesh['row'=4,'col'=4,'depth_0'=4,'depth_1'=2] {'row'}, dimensions={0}, use_global_device_ids=true | all-gather | bytes 327680 | tf_op jit(solution)/shard_map/all_gather | solution.py:167
  104.6 3.7 %all-gather.3 = f32[256,128]{0,1:T(8,128)S(1)} all-gather(f32[256,64]{0,1:T(8,128)S(1)} %slice.2), channel_id=5, replica_groups=mesh['row'=4,'col'=4,'depth_0'=4,'depth_1'=2] {'depth_1'}, dimensions={1}, use_global_device_ids=true | all-gather | bytes 196608 | tf_op jit(solution)/shard_map/all_gather | solution.py:179
  108.3 0.1 copy.29
  108.4 12.6 %all-gather.4.window = f32[256,512]{1,0:T(8,128)} all-gather(f32[256,128]{1,0:T(8,128)S(1)} %copy.29), channel_id=6, replica_groups=mesh['row'=4,'col'=4,'depth_0'=4,'depth_1'=2] {'depth_0'}, dimensions={1}, use_global_device_ids=true | all-gather | bytes 655360 | tf_op jit(solution)/shard_map/all_gather | solution.py:179
  121.0 0.0 all-to-all-done.4
  121.0 2.1 %copy.30.rows = f32[1008,512]{1,0:T(8,128)S(1)} copy(f32[1008,512]{0,1:T(8,128)} %bitcast.4) | data formatting | bytes 4128768 | tf_op jit(solution)/shard_map/all_to_all | solution.py:196
  123.1 1.0 copy-done
  124.1 1.0 copy-done.1
  125.2 1.2 copy-done.2
  126.4 26.1 %factor_solve_update.1 = (f32[4,512]{1,0:T(4,128)}, f32[252,512]{1,0:T(8,128)}, f32[1008,256]{1,0:T(8,128)}) custom-call(f32[512,512]{1,0:T(8,128)S(1)} %reshape_reshape.3.diag, f32[252,512]{1,0:T(8,128)S(1)} %copy-done.1, f32[1008,512]{1,0:T(8,128)S(1)} %copy.30.rows, f32[256,512]{1,0:T(8,128)S(1)} %copy-done, f32[1008,256]{1,0:T(8,128)S(1)} %copy-done.2), custom_call_target="tpu_custom_call" | custom-call | tf_op jit(solution)/shard_map/factor_solve_update/pallas_call | solution.py:135
  (4 shorter events, 0.0 us)
Async XLA Ops:
  0.6 16.2 %copy-start.3 = (f32[4,512]{1,0:T(4,128)S(1)}, f32[4,512]{1,0:T(4,128)}, u32[]{:S(2)}) copy-start(f32[4,512]{1,0:T(4,128)} %param.3) | copy-start | bytes 24580
  17.7 21.2 %all-to-all-start = ((f32[64,4,512]{2,1,0:T(4,128)}), f32[64,4,512]{2,1,0:T(4,128)S(1)}, u32[]{:S(2)}, u32[]{:S(2)}) async-start(f32[64,4,512]{2,1,0:T(4,128)} %broadcast_in_dim.9), calls=%async_computation | async-start | bytes 1048576 | tf_op jit(solution)/shard_map/all_to_all | solution.py:152
  67.3 16.0 %all-to-all-start.1 = ((f32[2,64,4,512]{3,2,1,0:T(4,128)}), f32[2,64,4,512]{3,2,1,0:T(4,128)S(1)}, u32[]{:S(2)}, u32[]{:S(2)}) async-start(f32[2,64,4,512]{3,2,1,0:T(4,128)} %broadcast_in_dim.10), calls=%async_computation.1 | async-start | bytes 2097152 | tf_op jit(solution)/shard_map/all_to_all | solution.py:152
  83.4 37.6 %all-to-all-start.4 = ((f32[8,1008,64]{1,2,0:T(8,128)}), f32[8,1008,64]{1,2,0:T(8,128)}, u32[]{:S(2)}, u32[]{:S(2)}) async-start(f32[8,1008,64]{1,2,0:T(8,128)} %copy.27), calls=%async_computation.4 | async-start | bytes 4194304 | tf_op jit(solution)/shard_map/all_to_all | solution.py:196
  123.1 1.0 copy-start
  124.1 1.0 copy-start.1
  125.2 1.2 copy-start.2
where the time goes:
time: 154 us; the launch traced here: 152 us
  blocking collectives  68.5 us (44%)
  Pallas kernels  26.1 us (17%)
  local copies, waits for them, and re-layouts  25.4 us (16%)
  starting transfers between devices  20.5 us (13%)
  waiting for transfers between devices  11.3 us (7%)
    all_to_all x1, blocking collectives, sent_to_all(): return lax.all_to_all(copies, axis, split_axis=0, concat_axis=0, tiled=True)  27.2 us
    pallas_call x1, Pallas kernels, all_compute(): pl.pallas_call(compute, out_shape=(jax.ShapeDtypeStruct((4, 512), F32), j...  26.1 us
    all_gather x2, blocking collectives, gathered_by_axis(): nearer = lax.all_gather(value, axes[-1], axis=dim, tiled=True)  16.2 us
    all_to_all x2, starting transfers between devices, sent_to_all(): return lax.all_to_all(copies, axis, split_axis=0, concat_axis=0, tiled=True)  16.2 us
    all_to_all x1, blocking collectives, split_panel(): lax.all_to_all(solved, DEPTH, split_axis=1, concat_axis=0, tiled=True)  14.9 us
    all_to_all x2, waiting for transfers between devices, sent_to_all(): return lax.all_to_all(copies, axis, split_axis=0, concat_axis=0, tiled=True)  11.3 us
    all_gather x1, blocking collectives, broadcast(): lax.all_gather(value, axis)  10.2 us
    all_to_all x3, local copies, waits for them, and re-layouts, body(): lax.all_to_all(row_panel, DEPTH, split_axis=0, concat_axis=1, tiled=True)  8.22 us
  transfers between devices with their start and end apart: 3, of which 1 were waited for; matrix products, arithmetic and copies ran while one was open for 9% of the time, Pallas kernels for 0%

commit v1 on v0

--- a/solution.py
+++ b/solution.py
@@ -3,13 +3,9 @@
 from jax import lax
 from jax.experimental import pallas as pl
 from jax.experimental.pallas import tpu as pltpu
-from jax.sharding import Mesh
 from jax.sharding import PartitionSpec as P
 
-DEPTH = ("depth_0", "depth_1")
-ROW_COL_DEPTH = ("row", "col", "depth_0", "depth_1")
-ROW_DEPTH = ("row", "depth_0", "depth_1")
-
+ALL = ("row", "col", "depth")
 
 F32 = jnp.float32
 NT = (((1,), (1,)), ((), ()))
@@ -114,10 +110,17 @@
     return total
 
 
-def compute(diag, own, rows, window, trailing, own_l, solved, updated, l_ref, s_ref):
+def compute(dbuf, own, rows, win, trailing, own_l, solved, updated, diag, window, l_ref, s_ref):
+    for p in range(128):
+        diag[4 * p : 4 * p + 4, :] = dbuf[p]
+    for s in range(8):
+        for r in range(4):
+            for u in range(2):
+                first = 32 * s + 8 * r + 4 * u
+                window[first : first + 4, :] = win[s, r, u]
     lows, invs = {}, {}
     factor_all(diag, l_ref, s_ref, lows, invs)
-    position = lax.axis_index("row") * 32 + lax.axis_index("col") * 8 + lax.axis_index(DEPTH)
+    position = (lax.axis_index("row") * 4 + lax.axis_index("col")) * 8 + lax.axis_index("depth")
     pair = l_ref[pl.ds(pl.multiple_of((position // 2) * 8, 8), 8), :]
     own_l[...] = jnp.where(position % 2 == 0, pair[0:4], pair[4:8])
     w = solve(window[...], lows, invs)
@@ -126,11 +129,11 @@
     size = own.shape[0]
     for j in range(4):
         span = slice(size * j, size * (j + 1))
-        x = solve(rows[span, :], lows, invs)
+        x = solve(rows[j], lows, invs)
         updated[span, :] = trailing[span, :] - product(x, w)
 
 
-def all_compute(diag, own, rows, window, trailing):
+def all_compute(dbuf, own, rows, win, trailing):
     spec = pl.BlockSpec(memory_space=pltpu.VMEM)
     return pl.pallas_call(
         compute,
@@ -141,72 +144,360 @@
         ),
         in_specs=[spec] * 5,
         out_specs=(spec,) * 3,
-        scratch_shapes=[pltpu.VMEM((512, 512), F32), pltpu.VMEM((512, 512), F32)],
-        compiler_params=pltpu.CompilerParams(vmem_limit_bytes=48 * 2**20),
+        scratch_shapes=[
+            pltpu.VMEM((512, 512), F32),
+            pltpu.VMEM((256, 512), F32),
+            pltpu.VMEM((512, 512), F32),
+            pltpu.VMEM((512, 512), F32),
+        ],
+        compiler_params=pltpu.CompilerParams(vmem_limit_bytes=36 * 2**20),
         name="factor_solve_update",
-    )(diag, own, rows, window, trailing)
-
-
-def sent_to_all(value, axis):
-    copies = jnp.broadcast_to(value, (lax.axis_size(axis), *value.shape))
-    return lax.all_to_all(copies, axis, split_axis=0, concat_axis=0, tiled=True)
-
-
-def in_order(tiles, dim):
-    shape = list(tiles.shape[1:])
-    shape[dim] *= tiles.shape[0]
-    return jnp.moveaxis(tiles, 0, dim).reshape(shape)
-
-
-def gather_directly(value, axis, dim):
-    tiles = sent_to_all(value, axis)
-    return in_order(tiles, dim)
-
-
-def broadcast(value, axis, root):
-    return lax.dynamic_index_in_dim(lax.all_gather(value, axis), root, 0, keepdims=False)
-
-
-def gather_axes(value, axes, dim):
-    far, near = axes
-    tiles = sent_to_all(sent_to_all(value, far), near)
-    return in_order(tiles.swapaxes(0, 1).reshape(-1, *value.shape), dim)
-
-
-def gathered_by_axis(value, axes, dim):
-    if not axes:
-        return value
-    nearer = lax.all_gather(value, axes[-1], axis=dim, tiled=True)
-    return gathered_by_axis(nearer, axes[:-1], dim)
-
-
-def split_panel(solved, win_rows):
-    ranges = lax.all_to_all(solved, DEPTH, split_axis=1, concat_axis=0, tiled=True)
-    row_panel = gather_directly(ranges, "col", 0)
-    local_window = lax.dynamic_slice_in_dim(
-        row_panel, lax.axis_index("col") * win_rows, win_rows, 0
+    )(dbuf, own, rows, win, trailing)
+
+
+def remote(src, dst, send, recv, **device):
+    return pltpu.make_async_remote_copy(
+        src_ref=src,
+        dst_ref=dst,
+        send_sem=send,
+        recv_sem=recv,
+        device_id=device,
+        device_id_type=pl.DeviceIdType.MESH,
     )
-    window = broadcast(local_window, "row", 0)
-    return (row_panel, window)
+
+
+class Exchange:
+    def __init__(self, diag, panel, dbuf, relay, rows, win, wsrc, pw, q, sems):
+        self.diag, self.panel, self.dbuf, self.relay, self.rows = diag, panel, dbuf, relay, rows
+        self.win, self.wsrc, self.pw, self.q = win, wsrc, pw, q
+        (self.loc, self.ds, self.dr, self.cs, self.cr, self.rs, self.rr, self.zs, self.zr, self.xs, self.xr,
+         self.w1s, self.w1r, self.w2s, self.w2r, self.w3s, self.w3r, self.w4s, self.w4r, self.w5s, self.w5r) = sems
+        self.r, self.c, self.s = (lax.axis_index(a) for a in ("row", "col", "depth"))
+        self.pos = (self.r * 4 + self.c) * 8 + self.s
+        self.corner = jnp.logical_and(self.r == 0, self.c == 0)
+
+    def enter(self):
+        r, c, s = self.r, self.c, self.s
+        self.own_diag = pltpu.make_async_copy(self.diag, self.dbuf.at[self.pos], self.loc.at[0])
+        self.own_panel = pltpu.make_async_copy(self.panel, self.relay.at[c], self.loc.at[1])
+        self.own_diag.start()
+        self.own_panel.start()
+        barrier = pltpu.get_barrier_semaphore()
+        for axis, me, n in (("depth", s, 8), ("col", c, 4), ("row", r, 4)):
+            for t in range(1, n):
+                pl.semaphore_signal(
+                    barrier, inc=1, device_id={axis: (me + t) % n}, device_id_type=pl.DeviceIdType.MESH
+                )
+        pl.semaphore_wait(barrier, 13)
+        self.own_diag.wait()
+
+    def diag_depth(self, t, pos):
+        ref = self.dbuf.at[pos]
+        return remote(ref, ref, self.ds.at[t], self.dr.at[t], depth=(self.s + t) % 8)
+
+    def diag_depth_send(self):
+        for t in range(1, 8):
+            self.diag_depth(t, self.pos).start()
+
+    def diag_depth_wait(self):
+        for t in range(1, 8):
+            self.diag_depth(t, (self.r * 4 + self.c) * 8 + (self.s - t) % 8).wait_recv()
+
+    def diag_col(self, t, c, i):
+        ref = self.dbuf.at[pl.ds(32 * i + 8 * c, 8), :, 0 : 128 * (i + 1)]
+        return remote(ref, ref, self.cs.at[t], self.cr.at[t], col=(self.c + t) % 4)
+
+    def diag_col_send(self):
+        for i in range(4):
+
+            @pl.when(self.r == i)
+            def _():
+                for t in range(1, 4):
+                    self.diag_col(t, self.c, i).start()
+
+    def diag_col_wait(self):
+        for i in range(4):
+
+            @pl.when(self.r == i)
+            def _():
+                for t in range(1, 4):
+                    self.diag_col(t, (self.c - t) % 4, i).wait_recv()
+
+    def diag_row(self, t, i):
+        ref = self.dbuf.at[32 * i : 32 * i + 32, :, 0 : 128 * (i + 1)]
+        return remote(ref, ref, self.rs.at[t], self.rr.at[t], row=(self.r + t) % 4)
+
+    def diag_row_send(self):
+        for i in range(4):
+
+            @pl.when(self.r == i)
+            def _():
+                for t in range(1, 4):
+                    self.diag_row(t, i).start()
+
+    def diag_row_wait(self, src):
+        for i in range(4):
+            if i != src:
+
+                @pl.when(self.r == i)
+                def _():
+                    self.diag_row((i - src) % 4, src).wait_recv()
+
+    def rows_col(self, k, slot, step, part):
+        ref = self.relay.at[slot]
+        if part is not None:
+            ref = self.relay.at[slot, :, 256 * part : 256 * part + 256]
+        return remote(ref, ref, self.zs.at[k], self.zr.at[k], col=(self.c + step) % 4)
+
+    def rows_col_send(self):
+        self.rows_col(0, self.c, 1, None).start()
+        self.rows_col(1, self.c, 3, None).start()
+
+    def rows_col_pass(self, k):
+        step = (1, 3)[k]
+        slot = (self.c - step) % 4
+        self.rows_col(k, slot, step, None).wait_recv()
+        self.rows_col(2 + k, slot, step, k).start()
+        self.rows_depth_send(1 + k, slot)
+
+    def rows_col_last(self):
+        slot = (self.c + 2) % 4
+        self.rows_col(2, slot, 1, 0).wait_recv()
+        self.rows_col(3, slot, 3, 1).wait_recv()
+        self.rows_depth_send(3, slot)
+
+    def rows_depth(self, k, slot):
+        target = 2 * slot + self.s // 4
+        return target, remote(
+            self.relay.at[slot], self.rows.at[self.s % 4], self.xs.at[k], self.xr.at[self.s % 4], depth=target
+        )
+
+    def rows_depth_send(self, k, slot):
+        target, copy = self.rows_depth(k, slot)
+
+        @pl.when(target != self.s)
+        def _():
+            copy.start()
+
+        @pl.when(target == self.s)
+        def _():
+            self.rows[self.s % 4] = self.relay[slot]
+
+    def rows_wait(self, j):
+        source = 4 * (self.s % 2) + j
+
+        @pl.when(source != self.s)
+        def _():
+            remote(
+                self.relay.at[0], self.rows.at[j], self.xs.at[0], self.xr.at[j], depth=source
+            ).wait_recv()
+
+    def win_main(self, i, d):
+        n = 8 if d < 7 else 7 - i
+        return remote(
+            self.wsrc.at[i + 8 * d : i + 8 * d + n], self.pw.at[i, 0:n], self.w1s.at[d], self.w1r.at[i], depth=d
+        )
+
+    def win_head(self, c):
+        return remote(self.wsrc.at[0 : c + 1], self.pw.at[c, 7 - c : 8], self.w1s.at[8], self.w1r.at[4 + c], depth=7)
+
+    def win_scatter(self, act):
+        for i in range(5):
+
+            @pl.when(jnp.logical_and(self.corner, self.s == i))
+            def _():
+                if i < 4:
+                    for d in range(8):
+                        if d != i:
+                            act(self.win_main(i, d))
+                if i > 0:
+                    act(self.win_head(i - 1))
+
+    def win_scatter_send(self):
+        self.own_panel.wait()
+
+        @pl.when(jnp.logical_and(self.corner, self.s < 5))
+        def _():
+            for u in range(63):
+                self.wsrc[u] = self.relay[0, 4 * u : 4 * u + 4, :]
+
+        for i in range(4):
+
+            @pl.when(jnp.logical_and(self.corner, self.s == i))
+            def _():
+                self.pw[i] = self.wsrc[9 * i : 9 * i + 8]
+
+        self.win_scatter(lambda copy: copy.start())
+
+    def win_scatter_wait(self):
+        for d in range(8):
+
+            @pl.when(jnp.logical_and(self.corner, self.s == d))
+            def _():
+                for i in range(4):
+                    if d != i:
+                        self.win_main(i, d).wait_recv()
+                    if d == 7:
+                        self.win_head(i).wait_recv()
+
+    def win_col(self, t):
+        return remote(self.pw.at[t], self.q, self.w2s.at[t], self.w2r.at[0], col=t)
+
+    def win_col_send(self):
+        @pl.when(self.corner)
+        def _():
+            for t in range(1, 4):
+                self.win_col(t).start()
+            self.q[...] = self.pw[0]
+
+    def win_col_wait(self):
+        @pl.when(jnp.logical_and(self.r == 0, self.c != 0))
+        def _():
+            self.win_col(1).wait_recv()
+
+    def win_row(self, t, row):
+        return remote(
+            self.q.at[2 * t : 2 * t + 2], self.win.at[self.s, row], self.w3s.at[t], self.w3r.at[0], row=t
+        )
+
+    def win_row_send(self):
+        @pl.when(self.r == 0)
+        def _():
+            for t in range(1, 4):
+                self.win_row(t, t).start()
+            self.win[self.s, 0] = self.q[0:2]
+
+    def win_row_wait(self):
+        @pl.when(self.r != 0)
+        def _():
+            self.win_row(1, self.r).wait_recv()
+
+    def win_depth(self, t, d):
+        ref = self.win.at[d, self.r]
+        return remote(ref, ref, self.w4s.at[t], self.w4r.at[t], depth=(self.s + t) % 8)
+
+    def win_depth_send(self):
+        for t in range(1, 8):
+            self.win_depth(t, self.s).start()
+
+    def win_depth_wait(self):
+        for t in range(1, 8):
+            self.win_depth(t, (self.s - t) % 8).wait_recv()
+
+    def win_all(self, t, row):
+        ref = self.win.at[:, row]
+        return remote(ref, ref, self.w5s.at[t], self.w5r.at[t], row=(self.r + t) % 4)
+
+    def win_all_send(self):
+        for t in range(1, 4):
+            self.win_all(t, self.r).start()
+
+    def win_all_wait(self):
+        for t in range(1, 4):
+            self.win_all(t, (self.r - t) % 4).wait_recv()
+
+    def leave(self):
+        for t in range(1, 8):
+            self.diag_depth(t, self.pos).wait_send()
+            self.win_depth(t, self.s).wait_send()
+        for i in range(4):
+
+            @pl.when(self.r == i)
+            def _():
+                for t in range(1, 4):
+                    self.diag_col(t, self.c, i).wait_send()
+                    self.diag_row(t, i).wait_send()
+
+        for t in range(1, 4):
+            self.win_all(t, self.r).wait_send()
+        for k in range(2):
+            step = (1, 3)[k]
+            self.rows_col(k, self.c, step, None).wait_send()
+            self.rows_col(2 + k, (self.c - step) % 4, step, k).wait_send()
+        for k, slot in enumerate((self.c, (self.c + 3) % 4, (self.c + 1) % 4, (self.c + 2) % 4)):
+            target, copy = self.rows_depth(k, slot)
+
+            @pl.when(target != self.s)
+            def _():
+                copy.wait_send()
+
+        self.win_scatter(lambda copy: copy.wait_send())
+
+        @pl.when(self.corner)
+        def _():
+            for t in range(1, 4):
+                self.win_col(t).wait_send()
+
+        @pl.when(self.r == 0)
+        def _():
+            for t in range(1, 4):
+                self.win_row(t, t).wait_send()
+
+
+SEMAPHORES = (2, 8, 8, 4, 4, 4, 4, 4, 4, 4, 4, 9, 8, 4, 1, 4, 1, 8, 8, 4, 4)
+
+
+def exchange(diag, panel, dbuf, rows, win, relay, wsrc, pw, q, *sems):
+    e = Exchange(diag, panel, dbuf, relay, rows, win, wsrc, pw, q, sems)
+    e.enter()
+    e.diag_depth_send()
+    e.win_scatter_send()
+    e.diag_depth_wait()
+    e.diag_col_send()
+    e.rows_col_send()
+    e.rows_depth_send(0, e.c)
+    e.win_scatter_wait()
+    e.win_col_send()
+    e.diag_col_wait()
+    e.diag_row_send()
+    e.win_col_wait()
+    e.win_row_send()
+    e.win_row_wait()
+    e.win_depth_send()
+    for i in range(4):
+        e.diag_row_wait(i)
+    e.rows_col_pass(0)
+    e.rows_col_pass(1)
+    e.win_depth_wait()
+    e.win_all_send()
+    e.rows_col_last()
+    e.win_all_wait()
+    for j in range(4):
+        e.rows_wait(j)
+    e.leave()
+
+
+def all_exchange(diag, panel):
+    vmem = pl.BlockSpec(memory_space=pltpu.VMEM)
+    hbm = pl.BlockSpec(memory_space=pltpu.HBM)
+    return pl.pallas_call(
+        exchange,
+        out_shape=(
+            jax.ShapeDtypeStruct((128, 4, 512), F32),
+            jax.ShapeDtypeStruct((4, *panel.shape), F32),
+            jax.ShapeDtypeStruct((8, 4, 2, 4, 512), F32),
+        ),
+        in_specs=[hbm, hbm],
+        out_specs=(vmem,) * 3,
+        scratch_shapes=[
+            pltpu.VMEM((4, *panel.shape), F32),
+            pltpu.VMEM((63, 4, 512), F32),
+            pltpu.VMEM((4, 8, 4, 512), F32),
+            pltpu.VMEM((8, 4, 512), F32),
+        ]
+        + [pltpu.SemaphoreType.DMA((n,)) for n in SEMAPHORES],
+        compiler_params=pltpu.CompilerParams(
+            collective_id=0, has_side_effects=True, vmem_limit_bytes=24 * 2**20
+        ),
+        name="exchange",
+    )(diag, panel)
 
 
 def body(diag_block, panel_rows, trailing):
-    whole_diag = gather_axes(diag_block, (("row", "col", "depth_0"), "depth_1"), 0)
-    row_panel, window = split_panel(panel_rows, trailing.shape[1])
-    owned = lax.all_to_all(row_panel, DEPTH, split_axis=0, concat_axis=1, tiled=True)
-    full_window = gathered_by_axis(window, DEPTH, 1)
-    return all_compute(whole_diag, panel_rows, owned, full_window, trailing)
+    dbuf, rows, win = all_exchange(diag_block, panel_rows)
+    return all_compute(dbuf, panel_rows, rows, win, trailing)
 
 
 def solution(mesh):
-    split = Mesh(
-        mesh.devices.reshape(mesh.shape["row"], mesh.shape["col"], 4, 2),
-        ("row", "col", "depth_0", "depth_1"),
-    )
-    return jax.shard_map(
-        body,
-        mesh=split,
-        in_specs=(P(ROW_COL_DEPTH, None), P(ROW_COL_DEPTH, None), P(ROW_DEPTH, "col")),
-        out_specs=(P(ROW_COL_DEPTH, None), P(ROW_COL_DEPTH, None), P(ROW_DEPTH, "col")),
-        check_vma=False,
-    )
+    specs = (P(ALL, None), P(ALL, None), P(("row", "depth"), "col"))
+    return jax.shard_map(body, mesh=mesh, in_specs=specs, out_specs=specs, check_vma=False)

time: 154 us -> 92.5 us (0.60)
  the two profiles are of different devices: /device:TPU:1 before, /device:TPU:54 now
where the time goes in v1:
time: 92.5 us; the launch traced here: 92.2 us
  Pallas kernels  87.6 us (95%)
  local copies, waits for them, and re-layouts  3.99 us (4%)
    pallas_call x1, Pallas kernels, all_exchange(): pl.pallas_call(exchange, out_shape=(jax.ShapeDtypeStruct((128, 4, 512), F...  61.6 us
    pallas_call x1, Pallas kernels, all_compute(): pl.pallas_call(compute, out_shape=(jax.ShapeDtypeStruct((4, 512), F32), j...  26 us
    unnamed x8, local copies, waits for them, and re-layouts  3.99 us

profile of v1, /device:TPU:54, one launch (start us, length us, event | category | flops | bytes accessed | tf_op | source)
XLA Modules:
  0.0 92.2 jit_solution(17992646881311772389)
XLA Ops:
  0.6 0.0 copy-start
  0.6 1.0 %copy-done = f32[252,512]{1,0:T(8,128)S(1)} copy-done((f32[252,512]{1,0:T(8,128)S(1)}, f32[252,512]{1,0:T(8,128)}, u32[]{:S(2)}) %copy-start) | copy-done | bytes 516120
  1.7 0.0 copy-start.3
  1.7 0.7 copy-done.3
  2.4 61.6 %exchange.1 = (f32[128,4,512]{2,1,0:T(4,128)S(1)}, f32[4,252,512]{2,1,0:T(8,128)S(1)}, f32[8,4,2,4,512]{4,3,2,1,0:T(4,128)S(1)}) custom-call(f32[4,512]{1,0:T(4,128)S(1)} %copy-done.3, f32[252,512]{1,0:T(8,128)S(1)} %copy-done), custom_call_target="tpu_custom_call" | custom-call | tf_op jit(solution)/shard_map/exchange/pallas_call | solution.py:473
  64.0 0.0 copy-start.1
  64.0 1.0 %copy-done.1 = f32[252,512]{1,0:T(8,128)S(1)} copy-done((f32[252,512]{1,0:T(8,128)S(1)}, f32[252,512]{1,0:T(8,128)}, u32[]{:S(2)}) %copy-start.1) | copy-done | bytes 516120
  65.0 0.0 copy-start.2
  65.0 1.2 %copy-done.2 = f32[1008,256]{1,0:T(8,128)S(1)} copy-done((f32[1008,256]{1,0:T(8,128)S(1)}, f32[1008,256]{1,0:T(8,128)}, u32[]{:S(2)}) %copy-start.2) | copy-done | bytes 1032216
  66.3 26.0 %factor_solve_update.1 = (f32[4,512]{1,0:T(4,128)}, f32[252,512]{1,0:T(8,128)}, f32[1008,256]{1,0:T(8,128)}) custom-call(f32[128,4,512]{2,1,0:T(4,128)S(1)} %get-tuple-element.6.dbuf, f32[252,512]{1,0:T(8,128)S(1)} %copy-done.1, f32[4,252,512]{2,1,0:T(8,128)S(1)} %get-tuple-element.7.rows, f32[8,4,2,4,512]{4,3,2,1,0:T(4,128)S(1)} %get-tuple-element.8.win, ...), custom_call_target="tpu_custom_call" | custom-call | tf_op jit(solution)/shard_map/factor_solve_update/pallas_call | solution.py:138
Async XLA Ops:
  0.6 1.0 %copy-start = (f32[252,512]{1,0:T(8,128)S(1)}, f32[252,512]{1,0:T(8,128)}, u32[]{:S(2)}) copy-start(f32[252,512]{1,0:T(8,128)} %own.1) | copy-start | bytes 1548292
  1.7 0.7 copy-start.3
  64.0 1.0 %copy-start.1 = (f32[252,512]{1,0:T(8,128)S(1)}, f32[252,512]{1,0:T(8,128)}, u32[]{:S(2)}) copy-start(f32[252,512]{1,0:T(8,128)} %own.1) | copy-start | bytes 1548292
  65.0 1.2 %copy-start.2 = (f32[1008,256]{1,0:T(8,128)S(1)}, f32[1008,256]{1,0:T(8,128)}, u32[]{:S(2)}) copy-start(f32[1008,256]{1,0:T(8,128)} %trailing.1) | copy-start | bytes 3096580
